TPU v7x, 32 devices: a whole 2x2x4 slice. The times are simulated.
32 devices in a mesh: ez: 4 (over z), ey: 2 (over y), ex: 4 (over x, core).
Axes of the slice: x: 2, y: 2, z: 4, core: 2. Of those that a mesh axis runs over, the one named last changes fastest.
Arguments:
- x_tokens: bfloat16 [16384, 2048], P(('ez', 'ey', 'ex'))
- expert_ids: int32 [16384, 4], P(('ez', 'ey', 'ex'))
- gate_vals: float32 [16384, 4], P(('ez', 'ey', 'ex'))
- w_gate: bfloat16 [32, 2048, 1792], P(('ex', 'ey', 'ez'))
- w_up: bfloat16 [32, 2048, 1792], P(('ex', 'ey', 'ez'))
- w_down: bfloat16 [32, 1792, 2048], P(('ex', 'ey', 'ez'))
Outputs:
- output: bfloat16 [16384, 2048], P(('ez', 'ey', 'ex'))
All inputs are finite; a program needn't handle non-finite values.
Results may differ from a plain program's by a relative error of at most 0.00585087.
Values are sent between devices in bfloat16 or wider.
A program may use at most 1 GiB of HBM per device.

v0:
```python
import jax
import jax.numpy as jnp
from jax import lax
from jax.sharding import PartitionSpec as P

TOKEN_AXES = ('ez', 'ey', 'ex')
EXPERT_AXES = ('ex', 'ey', 'ez')


def slot_layout(ids_local, n_exp, cap_slot):
    tok_dev, top_k = ids_local.shape
    flat_ids = ids_local.reshape(-1)
    match_mat = (flat_ids[:, None] == jnp.arange(n_exp)[None, :]).astype(jnp.int32)
    slot_rank = jnp.sum(jnp.cumsum(match_mat, axis=0) * match_mat, axis=1) - 1
    slot_idx = flat_ids * cap_slot + slot_rank
    pair_tok = jnp.arange(tok_dev * top_k, dtype=jnp.int32) // top_k
    slot_tok = jnp.zeros((n_exp * cap_slot,), jnp.int32).at[slot_idx].set(pair_tok)
    return slot_idx, slot_tok


def solution(mesh):
    n_dev = mesh.shape['ez'] * mesh.shape['ey'] * mesh.shape['ex']

    def local_layer(x_loc, ids_loc, gates_loc, w_g, w_u, w_d):
        tok_dev, hid_dim = x_loc.shape
        top_k = ids_loc.shape[1]
        n_local = w_g.shape[0]
        n_exp = n_local * n_dev
        cap_slot = 2 * tok_dev * top_k // n_exp
        slot_idx, slot_tok = slot_layout(ids_loc, n_exp, cap_slot)
        send_buf = jnp.take(x_loc, slot_tok, axis=0).reshape(n_dev, n_local, cap_slot, hid_dim)
        recv_buf = lax.all_to_all(send_buf, EXPERT_AXES, 0, 0)
        h_gate = jnp.einsum('slch,lhf->slcf', recv_buf, w_g, preferred_element_type=jnp.float32)
        h_up = jnp.einsum('slch,lhf->slcf', recv_buf, w_u, preferred_element_type=jnp.float32)
        act_bf = (jax.nn.silu(h_gate) * h_up).astype(jnp.bfloat16)
        exp_out = jnp.einsum('slcf,lfh->slch', act_bf, w_d, preferred_element_type=jnp.float32).astype(jnp.bfloat16)
        back_buf = lax.all_to_all(exp_out, EXPERT_AXES, 0, 0)
        back_flat = back_buf.reshape(n_exp * cap_slot, hid_dim)
        tok_rows = jnp.take(back_flat, slot_idx, axis=0).reshape(tok_dev, top_k, hid_dim)
        moe_sum = jnp.sum(gates_loc[:, :, None] * tok_rows, axis=1)
        return (x_loc.astype(jnp.float32) + moe_sum).astype(jnp.bfloat16)

    tok_spec = P(TOKEN_AXES, None)
    w_spec = P(EXPERT_AXES, None, None)
    return jax.shard_map(local_layer, mesh=mesh, in_specs=(tok_spec, tok_spec, tok_spec, w_spec, w_spec, w_spec), out_specs=tok_spec, check_vma=False)
```

profile of v0, /device:TPU:0, one launch (start us, length us, event | category | flops | bytes accessed | tf_op | source)
XLA Modules:
  0.0 974.1 jit_solution(4569434513189429088)
XLA Ops:
  0.0 1.0 copy.24
  1.0 0.2 eq.26
  1.2 0.2 reshape.116
  1.3 0.7 broadcast_multiply_fusion
  2.1 9.1 reduce-window.6
  11.1 0.1 slice.12
  11.3 0.2 copy.33
  11.5 0.2 reduce-window.9
  11.7 0.1 broadcast_add_fusion
  11.9 0.1 fusion.20
  12.0 0.1 copy.30
  12.1 0.2 mul.41
  12.3 0.0 copy-start.6
  12.4 0.6 copy-done.6
  12.9 8.1 scatter_custom_fusion
  21.1 21.0 %gather_fusion = bf16[4096,2048]{1,0:T(8,128)(2,1)} fusion(bf16[512,2048]{1,0:T(8,128)(2,1)S(1)} %copy-done, s32[4096]{0:T(1024)S(1)} %fusion.22), kind=kCustom, calls=%fused_computation | custom fusion | bytes 33570816 | tf_op jit(solution)/shard_map/jit(_take)/gather | solution.py:31
  42.0 8.5 broadcast_select_fusion
  50.5 376.6 %all_to_all.10 = bf16[32,1,128,2048]{3,2,1,0:T(8,128)(2,1)S(1)} all-to-all(bf16[32,1,128,2048]{3,2,1,0:T(8,128)(2,1)S(1)} %broadcast_select_fusion), channel_id=1, replica_groups=mesh['ez'=4,'ey'=2,'ex'=4] {'ex','ey','ez'}, dimensions={0} | all-to-all | bytes 33554432 | tf_op jit(solution)/shard_map/all_to_all | solution.py:32
  427.1 5.7 copy-done.2
  432.8 37.5 %fusion.4 = f32[32,128,1792]{2,1,0:T(8,128)} fusion(bf16[32,1,128,2048]{3,2,1,0:T(8,128)(2,1)S(1)} %all_to_all.10, bf16[1,2048,1792]{2,1,0:T(8,128)(2,1)} %param.10), kind=kOutput, calls=%fused_computation.10 | convolution fusion | flops 30064771072 | bytes 53477376 | tf_op jit(solution)/shard_map/slch,lhf->slcf/dot_general | solution.py:34
  470.4 41.5 %fusion.38 = bf16[32,128,1792]{2,1,0:T(8,128)(2,1)} fusion(f32[32,128,1792]{2,1,0:T(8,128)} %fusion.4, bf16[32,1,128,2048]{3,2,1,0:T(8,128)(2,1)} %copy-done.2, bf16[1,2048,1792]{2,1,0:T(8,128)(2,1)} %param.9), kind=kOutput, calls=%fused_computation.17.clone.clone.clone.1 | convolution fusion | flops 30108811264 | bytes 68157440 | tf_op jit(solution)/shard_map/slch,lhf->slcf/dot_general | solution.py:33
  511.8 37.2 %convert_bitcast_fusion = bf16[32,1,128,2048]{3,2,1,0:T(8,128)(2,1)} fusion(bf16[1,1792,2048]{2,1,0:T(8,128)(2,1)} %param.11, bf16[32,128,1792]{2,1,0:T(8,128)(2,1)} %fusion.38), kind=kOutput, calls=%fused_computation.14 | convolution fusion | flops 30073159680 | bytes 38797312 | tf_op jit(solution)/shard_map/slcf,lfh->slch/dot_general | solution.py:36
  549.0 7.1 all-to-all-start.1
  556.1 0.3 sub.15
  556.4 0.1 copy.28
  556.5 0.2 copy.29
  556.8 0.1 copy.23
  556.9 358.6 %all-to-all-done.1 = bf16[32,1,128,2048]{3,2,1,0:T(8,128)(2,1)} async-done(((bf16[32,1,128,2048]{3,2,1,0:T(8,128)(2,1)}), bf16[32,1,128,2048]{3,2,1,0:T(8,128)(2,1)}, u32[]{:S(2)}, u32[]{:S(2)}) %all-to-all-start.1) | async-done | bytes 16777248 | tf_op jit(solution)/shard_map/all_to_all | solution.py:37
  915.5 24.3 %gather_fusion.1 = bf16[2048,2048]{1,0:T(8,128)(2,1)} fusion(bf16[4096,2048]{1,0:T(8,128)(2,1)} %bitcast.28, s32[2048]{0:T(1024)S(1)} %broadcast_clamp_fusion), kind=kCustom, calls=%fused_computation.1 | custom fusion | bytes 16785408 | tf_op jit(solution)/shard_map/jit(_take)/gather | solution.py:39
  939.8 13.2 %gather.15 = bf16[512,4,2048]{2,1,0:T(4,128)(2,1)} reshape(bf16[2048,2048]{1,0:T(8,128)(2,1)} %gather_fusion.1) | data formatting | bytes 16777216 | tf_op jit(solution)/shard_map/jit(_take)/gather | solution.py:39
  953.0 19.0 %multiply_reduce_fusion = f32[512,2048]{1,0:T(8,128)S(1)} fusion(bf16[512,4,2048]{2,1,0:T(4,128)(2,1)} %gather.15, f32[512,4]{1,0:T(8,128)S(1)} %copy.23, pred[512,4]{1,0:T(8,128)(4,1)S(1)} %copy.29), kind=kLoop, calls=%fused_computation.13 | loop fusion | flops 15728640 | bytes 12593152 | tf_op jit(solution)/shard_map/reduce_sum | solution.py:40
  972.0 2.1 add_convert_fusion
  (23 shorter events, 0.1 us)
Async XLA Ops:
  0.0 21.0 %copy-start = (bf16[512,2048]{1,0:T(8,128)(2,1)S(1)}, bf16[512,2048]{1,0:T(8,128)(2,1)}, u32[]{:S(2)}) copy-start(bf16[512,2048]{1,0:T(8,128)(2,1)} %param.6) | copy-start | bytes 6291460
  12.0 30.0 %copy-start.3 = (s32[2048]{0:T(1024)}, s32[2048]{0:T(1024)S(1)}, u32[]{:S(2)}) copy-start(s32[2048]{0:T(1024)S(1)} %broadcast_add_fusion.1) | copy-start | bytes 24580
  12.3 0.6 copy-start.6
  427.1 5.7 copy-start.2
  549.0 7.2 copy-start.4
  549.0 7.5 copy-start.5
  549.0 7.8 copy-start.8
  549.0 7.9 copy-start.7
  549.0 366.5 %all-to-all-start.1 = ((bf16[32,1,128,2048]{3,2,1,0:T(8,128)(2,1)}), bf16[32,1,128,2048]{3,2,1,0:T(8,128)(2,1)}, u32[]{:S(2)}, u32[]{:S(2)}) async-start(bf16[32,1,128,2048]{3,2,1,0:T(8,128)(2,1)} %convert_bitcast_fusion), calls=%async_computation.1 | async-start | bytes 33554432 | tf_op jit(solution)/shard_map/all_to_all | solution.py:37
  939.7 32.3 %copy-start.1 = (bf16[512,2048]{1,0:T(8,128)(2,1)S(1)}, bf16[512,2048]{1,0:T(8,128)(2,1)}, u32[]{:S(2)}) copy-start(bf16[512,2048]{1,0:T(8,128)(2,1)} %param.6) | copy-start | bytes 6291460
where the time goes:
time: 989 us; the launch traced here: 974 us
  blocking collectives  377 us (38%)
  waiting for transfers between devices  359 us (36%)
  matrix products  116 us (12%)
  local copies, waits for them, and re-layouts  75.6 us (8%)
  other arithmetic  39.9 us (4%)
    all_to_all x1, blocking collectives, local_layer(): recv_buf = lax.all_to_all(send_buf, EXPERT_AXES, 0, 0)  377 us
    all_to_all x1, waiting for transfers between devices, local_layer(): back_buf = lax.all_to_all(exp_out, EXPERT_AXES, 0, 0)  359 us
    dot_general x1, matrix products, local_layer(): jnp.einsum('slch,lhf->slcf', recv_buf, w_g, preferred_element_type=jnp.fl...  41.5 us
    dot_general x1, matrix products, local_layer(): jnp.einsum('slch,lhf->slcf', recv_buf, w_u, preferred_element_type=jnp.fl...  37.5 us
    gather x2, local copies, waits for them, and re-layouts, local_layer(): jnp.take(back_flat, slot_idx, axis=0).reshape(tok_dev, top_k, hid_dim)  37.5 us
    dot_general x1, matrix products, local_layer(): jnp.einsum('slcf,lfh->slch', act_bf, w_d, preferred_element_type=jnp.floa...  37.2 us
    gather x1, local copies, waits for them, and re-layouts, local_layer(): jnp.take(x_loc, slot_tok, axis=0).reshape(n_dev, n_local, cap_slot, hid_dim)  21 us
  transfers between devices with their start and end apart: 1, of which 1 were waited for; matrix products, arithmetic and copies ran while one was open for 0% of the time, Pallas kernels for 0%

commit v1 on v0

v1 whole, which is shorter than its diff:
```python
import jax
import jax.numpy as jnp
from jax import lax
from jax.experimental import pallas as pl
from jax.experimental.pallas import tpu as pltpu
from jax.sharding import PartitionSpec as P

TOKEN_AXES = ('ez', 'ey', 'ex')
EXPERT_AXES = ('ex', 'ey', 'ez')
MESH = pl.DeviceIdType.MESH
BF16 = jnp.bfloat16
F32 = jnp.float32
SEND_ORDER = (6, 7, 2, 3, 4, 5, 1)


def tile_of(n):
    return 256 if n % 256 == 0 else 128


def z_peer(k):
    z = lax.axis_index('ez')
    return 2 * ((z // 2 + k // 2) % 2) + (z % 2 + k % 2) % 2


def plane_peer(j):
    y, col = lax.axis_index('ey'), lax.axis_index('ex')
    return (y + j // 4) % 2, 2 * ((col // 2 + (j // 2) % 2) % 2) + (col % 2 + j % 2) % 2


def moe_kernel(x_ref, rkr_ref, rg_ref, w1_ref, w3_ref, w2_ref,
               y_ref, xz_ref, dr_ref, rr_ref, zr_ref,
               w1v, w3v, w2v, gbuf, rbuf, act, xbuf, sel, cmat, pb,
               w_sem, xl_sem, rl_sem, pl_sem, xs_sem, xr_sem, ds_sem, dr_sem, rs_sem, rc_sem, zs_sem, zr_sem):
    tok, hid = x_ref.shape
    ffn = w1_ref.shape[1]
    rows = gbuf.shape[1]
    cap = rows // 8
    half = rows // 2
    pieces = xs_sem.shape[1]
    prow = tok // pieces
    tn, tf = tile_of(hid), tile_of(ffn)
    tt = cmat.shape[1]

    def xcopy(k, p):
        span = pl.ds(p * prow, prow)
        src = xz_ref.at[1, span] if k == 3 else x_ref.at[span]
        return pltpu.make_async_remote_copy(
            src_ref=src, dst_ref=xz_ref.at[k - 1, span], send_sem=xs_sem.at[k, p], recv_sem=xr_sem.at[k, p],
            device_id={'ez': z_peer(1 if k == 3 else k)}, device_id_type=MESH)

    def plane_copy(src, dst, k, j, send, recv):
        span = pl.ds(j * cap, cap)
        if j == 0:
            return pltpu.make_async_copy(src.at[k, span], dst.at[k, span], recv.at[k, 0])
        yy, cc = plane_peer(j)
        return pltpu.make_async_remote_copy(
            src_ref=src.at[k, span], dst_ref=dst.at[k, span], send_sem=send.at[k, j], recv_sem=recv.at[k, j],
            device_id={'ey': yy, 'ex': cc}, device_id_type=MESH)

    def dcopy(k, j):
        return plane_copy(gbuf, dr_ref, k, j, ds_sem, dr_sem)

    def rcopy(k, j):
        return plane_copy(gbuf, rr_ref, k, j, rs_sem, rc_sem)

    def zcopy(slot, i, k):
        return pltpu.make_async_remote_copy(
            src_ref=pb.at[slot], dst_ref=zr_ref.at[i], send_sem=zs_sem.at[i], recv_sem=zr_sem.at[i],
            device_id={'ez': z_peer(k)}, device_id_type=MESH)

    def wait_recv(copy, j):
        if j == 0:
            copy.wait()
        else:
            copy.wait_recv()

    weights = [pltpu.make_async_copy(s, d, w_sem.at[i])
               for i, (s, d) in enumerate(((w1_ref, w1v), (w3_ref, w3v), (w2_ref, w2v)))]

    def load_x(k):
        return pltpu.make_async_copy(x_ref if k == 0 else xz_ref.at[k - 1], xbuf, xl_sem)

    def gather(k):
        load = load_x(k)
        load.start()
        s = z_peer(k)
        for j in range(8):
            slot = lax.broadcasted_iota(jnp.int32, (cap, tok), 0).astype(F32)
            hit = rkr_ref[s, j:j + 1, :] == slot
            sel[j * cap:(j + 1) * cap, :] = jnp.where(hit, 1.0, 0.0).astype(BF16)
        load.wait()

        def body(n, carry):
            cols = pl.ds(pl.multiple_of(n * tn, tn), tn)
            gbuf[k, :, cols] = jnp.dot(sel[...], xbuf[:, cols], preferred_element_type=F32).astype(BF16)
            return carry

        lax.fori_loop(0, hid // tn, body, 0)
        for j in SEND_ORDER + (0,):
            dcopy(k, j).start()

    def expert(k):
        loads = []
        for h in range(2):
            for j in range(4 * h, 4 * h + 4):
                wait_recv(dcopy(k, j), j)
            span = pl.ds(h * half, half)
            loads.append(pltpu.make_async_copy(dr_ref.at[k, span], rbuf.at[span], rl_sem.at[h]))
            loads[h].start()
        for j in range(1, 8):
            dcopy(k, j).wait_send()
        for h in range(2):
            loads[h].wait()
            span = pl.ds(h * half, half)

            def up(n, carry):
                cols = pl.ds(pl.multiple_of(n * tf, tf), tf)
                row = rbuf[span, :]
                one = jnp.dot(row, w1v[:, cols], preferred_element_type=F32)
                three = jnp.dot(row, w3v[:, cols], preferred_element_type=F32)
                act[:, cols] = (one * jax.nn.sigmoid(one) * three).astype(BF16)
                return carry

            lax.fori_loop(0, ffn // tf, up, 0)

            def down(n, carry):
                cols = pl.ds(pl.multiple_of(n * tn, tn), tn)
                gbuf[k, span, cols] = jnp.dot(act[...], w2v[:, cols], preferred_element_type=F32).astype(BF16)
                return carry

            lax.fori_loop(0, hid // tn, down, 0)

    def send_back(k):
        for j in SEND_ORDER + (0,):
            rcopy(k, j).start()

    def combine(k, slot):
        loads = []
        for h in range(2):
            for j in range(4 * h, 4 * h + 4):
                wait_recv(rcopy(k, j), j)
            span = pl.ds(h * half, half)
            loads.append(pltpu.make_async_copy(rr_ref.at[k, span], rbuf.at[span], rl_sem.at[h]))
            loads[h].start()
        s = z_peer(k)
        for t in range(tok // tt):
            span = pl.ds(t * tt, tt)
            info = rg_ref[s, span, :]
            for j in range(8):
                slots = lax.broadcasted_iota(jnp.int32, (tt, cap), 1).astype(F32)
                hit = info[:, j:j + 1] == slots
                left = info[:, 8 + j:9 + j]
                for i in range(3):
                    part = left.astype(BF16).astype(F32)
                    left = left - part
                    cmat[i, :, j * cap:(j + 1) * cap] = jnp.where(hit, part, 0.0).astype(BF16)
            if t == 0:
                for load in loads:
                    load.wait()

            def body(n, carry):
                cols = pl.ds(pl.multiple_of(n * tn, tn), tn)
                back = rbuf[:, cols]
                total = jnp.dot(cmat[2], back, preferred_element_type=F32)
                total = total + jnp.dot(cmat[1], back, preferred_element_type=F32)
                pb[slot, span, cols] = total + jnp.dot(cmat[0], back, preferred_element_type=F32)
                return carry

            lax.fori_loop(0, hid // tn, body, 0)

    for k in (1, 2):
        for p in range(pieces):
            xcopy(k, p).start()
    for w in weights:
        w.start()
    gather(0)
    for p in range(pieces):
        xcopy(1, p).wait_recv()
    gather(1)
    for w in weights:
        w.wait()
    expert(0)
    for p in range(pieces):
        xcopy(2, p).wait_recv()
        xcopy(3, p).start()
    gather(2)
    expert(1)
    for p in range(pieces):
        xcopy(3, p).wait_recv()
    gather(3)
    expert(2)
    expert(3)
    for k in (3, 1, 2, 0):
        send_back(k)
    combine(3, 0)
    zcopy(0, 1, 1).start()
    combine(1, 2)
    zcopy(2, 0, 1).start()
    combine(2, 1)
    zcopy(0, 1, 1).wait()
    near = pltpu.make_async_copy(zr_ref.at[1], pb.at[0], pl_sem.at[0])
    near.start()
    near.wait()

    def row_loop(body):
        step = 16
        lax.fori_loop(0, tok // step, lambda i, c: (body(pl.ds(pl.multiple_of(i * step, step), step)), c)[1], 0)

    def add_near(span):
        pb[1, span, :] += pb[0, span, :]

    row_loop(add_near)
    zcopy(1, 2, 2).start()
    combine(0, 0)
    load = load_x(0)
    load.start()
    load.wait()
    zcopy(2, 0, 1).wait()
    first = pltpu.make_async_copy(zr_ref.at[0], pb.at[2], pl_sem.at[1])
    first.start()
    first.wait()

    def add_first(span):
        pb[0, span, :] += xbuf[span, :].astype(F32) + pb[2, span, :]

    row_loop(add_first)
    zcopy(1, 2, 2).wait()
    last = pltpu.make_async_copy(zr_ref.at[2], pb.at[1], pl_sem.at[0])
    last.start()
    last.wait()

    def add_last(span):
        xbuf[span, :] = (pb[0, span, :] + pb[1, span, :]).astype(BF16)

    row_loop(add_last)
    out = pltpu.make_async_copy(xbuf, y_ref, xl_sem)
    out.start()
    for k in (1, 2, 3):
        for p in range(pieces):
            xcopy(k, p).wait_send()
    for k in range(4):
        for j in range(1, 8):
            rcopy(k, j).wait_send()
    out.wait()


def route(ids, gates):
    tok = ids.shape[0]
    peers = [plane_peer(j) for j in range(8)]
    experts = jnp.stack([(c * 2 + y) * 4 + z for z in range(4) for y, c in peers]).astype(jnp.int32)
    match = ids[:, :, None] == experts[None, None, :]
    picked = jnp.any(match, axis=1)
    gate = jnp.sum(jnp.where(match, gates[:, :, None], 0.0), axis=1)
    at = jnp.arange(tok)
    before = (at[None, :] < at[:, None]).astype(BF16)
    rank = jnp.dot(before, picked.astype(BF16), preferred_element_type=F32)
    rank = jnp.where(picked, rank, -1.0)
    info = jnp.concatenate([rank.reshape(tok, 4, 8), gate.reshape(tok, 4, 8)], axis=2)
    return lax.all_to_all(info.transpose(1, 0, 2), 'ez', 0, 0)


def solution(mesh):
    n_dev = mesh.shape['ez'] * mesh.shape['ey'] * mesh.shape['ex']

    def local_layer(x_loc, ids_loc, gates_loc, w_g, w_u, w_d):
        tok, hid = x_loc.shape
        ffn = w_g.shape[2]
        cap = 2 * tok * ids_loc.shape[1] // n_dev
        rows = 8 * cap
        info = route(ids_loc, gates_loc)
        ranks = info[:, :, :8].transpose(0, 2, 1)
        pieces = 2
        any_spec = pl.BlockSpec(memory_space=pl.ANY)
        vmem_spec = pl.BlockSpec(memory_space=pltpu.VMEM)
        dma = pltpu.SemaphoreType.DMA
        outs = pl.pallas_call(
            moe_kernel,
            out_shape=(
                jax.ShapeDtypeStruct((tok, hid), BF16),
                jax.ShapeDtypeStruct((3, tok, hid), BF16),
                jax.ShapeDtypeStruct((4, rows, hid), BF16),
                jax.ShapeDtypeStruct((4, rows, hid), BF16),
                jax.ShapeDtypeStruct((3, tok, hid), F32),
            ),
            in_specs=[any_spec, vmem_spec, vmem_spec, any_spec, any_spec, any_spec],
            out_specs=(any_spec,) * 5,
            scratch_shapes=[
                pltpu.VMEM((hid, ffn), BF16),
                pltpu.VMEM((hid, ffn), BF16),
                pltpu.VMEM((ffn, hid), BF16),
                pltpu.VMEM((4, rows, hid), BF16),
                pltpu.VMEM((rows, hid), BF16),
                pltpu.VMEM((rows // 2, ffn), BF16),
                pltpu.VMEM((tok, hid), BF16),
                pltpu.VMEM((rows, tok), BF16),
                pltpu.VMEM((3, tok // 2, rows), BF16),
                pltpu.VMEM((3, tok, hid), F32),
                dma((3,)), dma, dma((2,)), dma((2,)),
                dma((4, pieces)), dma((4, pieces)),
                dma((4, 8)), dma((4, 8)), dma((4, 8)), dma((4, 8)),
                dma((3,)), dma((3,)),
            ],
            compiler_params=pltpu.CompilerParams(has_side_effects=True, vmem_limit_bytes=67043328),
        )(x_loc, ranks, info, w_g[0], w_u[0], w_d[0])
        return outs[0]

    tok_spec = P(TOKEN_AXES, None)
    w_spec = P(EXPERT_AXES, None, None)
    return jax.shard_map(local_layer, mesh=mesh, in_specs=(tok_spec, tok_spec, tok_spec, w_spec, w_spec, w_spec), out_specs=tok_spec, check_vma=False)
```

time: 989 us -> 630 us (0.64); the launches traced: 974 us -> 630 us
  Pallas kernels: 0 us -> 610 us
  blocking collectives: 377 us -> 12.9 us
  waiting for transfers between devices: 359 us -> 0 us
  matrix products: 116 us -> 0.24 us
  local copies, waits for them, and re-layouts: 75.6 us -> 5.21 us
  other arithmetic: 39.9 us -> 1.65 us
    pallas_call x0 -> x1, Pallas kernels: none -> 610 us  [local_layer(): pl.pallas_call(moe_kernel, out_shape=(jax.ShapeDtypeStruct((tok, hid), BF...]
    all_to_all x1, blocking collectives: 377 us -> 12.9 us  [route(): return lax.all_to_all(info.transpose(1, 0, 2), 'ez', 0, 0)]
    all_to_all x1 -> x0, waiting for transfers between devices: 359 us -> none  [local_layer(): back_buf = lax.all_to_all(exp_out, EXPERT_AXES, 0, 0)]
    dot_general x3 -> x1, matrix products: 116 us -> 0.24 us  [route(): rank = jnp.dot(before, picked.astype(BF16), preferred_element_type=F32)]
    gather x3 -> x0, local copies, waits for them, and re-layouts: 58.5 us -> none  [the longest x2 37.5 us: local_layer(): jnp.take(back_flat, slot_idx, axis=0).reshape(tok_dev, top_k, hid_dim)]
    reduce_sum x2 -> x1, other arithmetic: 19.1 us -> 0.84 us  [route(): gate = jnp.sum(jnp.where(match, gates[:, :, None], 0.0), axis=1)]
  transfers between devices with their start and end apart: 1 -> 0, of which waited for: 1 -> 0; matrix products, arithmetic and copies ran while one was open for 0% -> 0% of each run, Pallas kernels for 0% -> 0%
where the time goes in v1:
time: 630 us
  Pallas kernels  610 us (97%)
  blocking collectives  12.9 us (2%)
    pallas_call x1, Pallas kernels, local_layer(): pl.pallas_call(moe_kernel, out_shape=(jax.ShapeDtypeStruct((tok, hid), BF...  610 us
    all_to_all x1, blocking collectives, route(): return lax.all_to_all(info.transpose(1, 0, 2), 'ez', 0, 0)  12.9 us

profile of v1, /device:TPU:0, one launch (start us, length us, event | category | flops | bytes accessed | tf_op | source)
XLA Modules:
  0.0 629.8 jit_solution(13988035813198518014)
XLA Ops:
  0.0 0.1 stack.131
  0.1 0.8 compare_reduce_fusion
  0.9 0.2 fusion
  1.2 0.8 fusion.1
  2.0 12.9 %all_to_all.5 = f32[4,512,16]{1,2,0:T(8,128)S(1)} all-to-all(f32[4,512,16]{1,2,0:T(8,128)S(1)} %maximum_bitcast_fusion), channel_id=1, replica_groups=mesh['ez'=4,'ey'=2,'ex'=4] {'ez'}, dimensions={0} | all-to-all | bytes 262144 | tf_op jit(solution)/shard_map/all_to_all | solution.py:259
  14.9 0.6 slice_bitcast_fusion.rkr_ref
  15.5 1.3 copy.18.rg_ref
  16.8 609.8 %shard_map.64 = (bf16[512,2048]{1,0:T(8,128)(2,1)}, bf16[3,512,2048]{2,1,0:T(8,128)(2,1)}, bf16[4,1024,2048]{2,1,0:T(8,128)(2,1)}, bf16[4,1024,2048]{2,1,0:T(8,128)(2,1)}, f32[3,512,2048]{2,1,0:T(8,128)}) custom-call(bf16[512,2048]{1,0:T(8,128)(2,1)} %x_ref.1, f32[4,8,512]{2,1,0:T(8,128)} %slice_bitcast_fusion.rkr_ref, f32[4,512,16]{2,1,0:T(8,128)} %copy.18.rg_ref, ...), custom_call_target="tpu_custom_call" | custom-call | tf_op jit(solution)/shard_map/pallas_call | solution.py:276
  626.7 3.2 copy.20
  (1 shorter events, 0.0 us)

commit v2 on v1

--- a/solution.py
+++ b/solution.py
@@ -10,7 +10,8 @@
 MESH = pl.DeviceIdType.MESH
 BF16 = jnp.bfloat16
 F32 = jnp.float32
-SEND_ORDER = (6, 7, 2, 3, 4, 5, 1)
+OFFSET = (0, 1, 2, 4, 3, 5, 6, 7)
+HALVES = ((2, 3, 1, 0), (4, 5, 6, 7))
 
 
 def tile_of(n):
@@ -24,13 +25,14 @@
 
 def plane_peer(j):
     y, col = lax.axis_index('ey'), lax.axis_index('ex')
+    j = OFFSET[j]
     return (y + j // 4) % 2, 2 * ((col // 2 + (j // 2) % 2) % 2) + (col % 2 + j % 2) % 2
 
 
 def moe_kernel(x_ref, rkr_ref, rg_ref, w1_ref, w3_ref, w2_ref,
                y_ref, xz_ref, dr_ref, rr_ref, zr_ref,
                w1v, w3v, w2v, gbuf, rbuf, act, xbuf, sel, cmat, pb,
-               w_sem, xl_sem, rl_sem, pl_sem, xs_sem, xr_sem, ds_sem, dr_sem, rs_sem, rc_sem, zs_sem, zr_sem):
+               w_sem, xl_sem, rl_sem, pl_sem, xs_sem, xr_sem, ds_sem, dr_sem, rs_sem, rc_sem, zs_sem, zr_sem, out_sem):
     tok, hid = x_ref.shape
     ffn = w1_ref.shape[1]
     rows = gbuf.shape[1]
@@ -40,6 +42,10 @@
     prow = tok // pieces
     tn, tf = tile_of(hid), tile_of(ffn)
     tt = cmat.shape[1]
+    parts = tok // tt
+    z = lax.axis_index('ez')
+    inner = ((z + 1) // 2) % 2
+    first, second = 1 + inner, 2 - inner
 
     def xcopy(k, p):
         span = pl.ds(p * prow, prow)
@@ -63,10 +69,17 @@
     def rcopy(k, j):
         return plane_copy(gbuf, rr_ref, k, j, rs_sem, rc_sem)
 
-    def zcopy(slot, i, k):
+    def zcopy(slot, i, k, t):
+        span = pl.ds(t * tt, tt)
         return pltpu.make_async_remote_copy(
-            src_ref=pb.at[slot], dst_ref=zr_ref.at[i], send_sem=zs_sem.at[i], recv_sem=zr_sem.at[i],
+            src_ref=pb.at[slot, span], dst_ref=zr_ref.at[i, span], send_sem=zs_sem.at[i, t], recv_sem=zr_sem.at[i, t],
             device_id={'ez': z_peer(k)}, device_id_type=MESH)
+
+    def wait_x(k, p):
+        span = pl.ds(p * prow, prow)
+        pltpu.make_async_remote_copy(
+            src_ref=x_ref.at[span], dst_ref=xz_ref.at[k - 1, span], send_sem=xs_sem.at[k, p], recv_sem=xr_sem.at[k, p],
+            device_id={'ez': z_peer(k)}, device_id_type=MESH).wait_recv()
 
     def wait_recv(copy, j):
         if j == 0:
@@ -77,11 +90,11 @@
     weights = [pltpu.make_async_copy(s, d, w_sem.at[i])
                for i, (s, d) in enumerate(((w1_ref, w1v), (w3_ref, w3v), (w2_ref, w2v)))]
 
-    def load_x(k):
-        return pltpu.make_async_copy(x_ref if k == 0 else xz_ref.at[k - 1], xbuf, xl_sem)
-
-    def gather(k):
-        load = load_x(k)
+    def load_x(own, k):
+        return pltpu.make_async_copy(x_ref if own else xz_ref.at[k - 1], xbuf, xl_sem)
+
+    def gather(k, own=False):
+        load = load_x(own, k)
         load.start()
         s = z_peer(k)
         for j in range(8):
@@ -96,10 +109,10 @@
             return carry
 
         lax.fori_loop(0, hid // tn, body, 0)
-        for j in SEND_ORDER + (0,):
+        for j in HALVES[0] + HALVES[1]:
             dcopy(k, j).start()
 
-    def expert(k):
+    def expert(k, send=False):
         loads = []
         for h in range(2):
             for j in range(4 * h, 4 * h + 4):
@@ -129,21 +142,17 @@
                 return carry
 
             lax.fori_loop(0, hid // tn, down, 0)
-
-    def send_back(k):
-        for j in SEND_ORDER + (0,):
+            if send:
+                send_back(k, h)
+
+    def send_back(k, h):
+        for j in HALVES[h]:
             rcopy(k, j).start()
 
-    def combine(k, slot):
+    def combine(k, slot, then, done):
+        s = z_peer(k)
         loads = []
-        for h in range(2):
-            for j in range(4 * h, 4 * h + 4):
-                wait_recv(rcopy(k, j), j)
-            span = pl.ds(h * half, half)
-            loads.append(pltpu.make_async_copy(rr_ref.at[k, span], rbuf.at[span], rl_sem.at[h]))
-            loads[h].start()
-        s = z_peer(k)
-        for t in range(tok // tt):
+        for t in range(parts):
             span = pl.ds(t * tt, tt)
             info = rg_ref[s, span, :]
             for j in range(8):
@@ -155,6 +164,13 @@
                     left = left - part
                     cmat[i, :, j * cap:(j + 1) * cap] = jnp.where(hit, part, 0.0).astype(BF16)
             if t == 0:
+                for h in range(2):
+                    for j in range(4 * h, 4 * h + 4):
+                        wait_recv(rcopy(k, j), j)
+                    rspan = pl.ds(h * half, half)
+                    loads.append(pltpu.make_async_copy(rr_ref.at[k, rspan], rbuf.at[rspan], rl_sem.at[h]))
+                    loads[h].start()
+                then()
                 for load in loads:
                     load.wait()
 
@@ -167,81 +183,107 @@
                 return carry
 
             lax.fori_loop(0, hid // tn, body, 0)
-
-    for k in (1, 2):
+            done(t)
+
+    def row_loop(t, body):
+        step = 16
+        lax.fori_loop(
+            0, tt // step, lambda i, c: (body(pl.ds(pl.multiple_of(t * tt + i * step, step), step)), c)[1], 0)
+
+    def fetch(i, slot, t):
+        span = pl.ds(t * tt, tt)
+        return pltpu.make_async_copy(zr_ref.at[i, span], pb.at[slot, span], pl_sem.at[t])
+
+    @pl.when(inner == 0)
+    def _():
         for p in range(pieces):
-            xcopy(k, p).start()
+            xcopy(2, p).start()
+
+    for p in range(pieces):
+        xcopy(1, p).start()
     for w in weights:
         w.start()
-    gather(0)
+    gather(0, own=True)
     for p in range(pieces):
-        xcopy(1, p).wait_recv()
-    gather(1)
+        wait_x(first, p)
+
+    @pl.when(inner == 1)
+    def _():
+        for p in range(pieces):
+            xcopy(2, p).start()
+
+    gather(first)
     for w in weights:
         w.wait()
     expert(0)
     for p in range(pieces):
-        xcopy(2, p).wait_recv()
+        wait_x(second, p)
         xcopy(3, p).start()
-    gather(2)
-    expert(1)
+    gather(second)
+    expert(first)
     for p in range(pieces):
-        xcopy(3, p).wait_recv()
+        wait_x(3, p)
     gather(3)
-    expert(2)
-    expert(3)
-    for k in (3, 1, 2, 0):
-        send_back(k)
-    combine(3, 0)
-    zcopy(0, 1, 1).start()
-    combine(1, 2)
-    zcopy(2, 0, 1).start()
-    combine(2, 1)
-    zcopy(0, 1, 1).wait()
-    near = pltpu.make_async_copy(zr_ref.at[1], pb.at[0], pl_sem.at[0])
-    near.start()
-    near.wait()
-
-    def row_loop(body):
-        step = 16
-        lax.fori_loop(0, tok // step, lambda i, c: (body(pl.ds(pl.multiple_of(i * step, step), step)), c)[1], 0)
-
-    def add_near(span):
-        pb[1, span, :] += pb[0, span, :]
-
-    row_loop(add_near)
-    zcopy(1, 2, 2).start()
-    combine(0, 0)
-    load = load_x(0)
+    expert(second)
+    expert(3, send=True)
+
+    def back(k):
+        return lambda: [send_back(k, h) for h in range(2)] and None
+
+    combine(3, 0, back(1), lambda t: zcopy(0, 1, 1, t).start())
+    combine(1, 2, back(2), lambda t: zcopy(2, 0, 1, t).start())
+
+    def pass_on(t):
+        zcopy(0, 1, 1, t).wait()
+        near = fetch(1, 0, t)
+        near.start()
+        near.wait()
+
+        def add_near(span):
+            pb[1, span, :] += pb[0, span, :]
+
+        row_loop(t, add_near)
+        zcopy(1, 2, 2, t).start()
+
+    combine(2, 1, back(0), pass_on)
+    load = load_x(True, 0)
     load.start()
+    combine(0, 0, lambda: None, lambda t: None)
     load.wait()
-    zcopy(2, 0, 1).wait()
-    first = pltpu.make_async_copy(zr_ref.at[0], pb.at[2], pl_sem.at[1])
-    first.start()
-    first.wait()
-
-    def add_first(span):
-        pb[0, span, :] += xbuf[span, :].astype(F32) + pb[2, span, :]
-
-    row_loop(add_first)
-    zcopy(1, 2, 2).wait()
-    last = pltpu.make_async_copy(zr_ref.at[2], pb.at[1], pl_sem.at[0])
-    last.start()
-    last.wait()
-
-    def add_last(span):
-        xbuf[span, :] = (pb[0, span, :] + pb[1, span, :]).astype(BF16)
-
-    row_loop(add_last)
-    out = pltpu.make_async_copy(xbuf, y_ref, xl_sem)
-    out.start()
+    for t in range(parts):
+        zcopy(2, 0, 1, t).wait()
+        near = fetch(0, 2, t)
+        near.start()
+        near.wait()
+
+        def add_first(span):
+            pb[0, span, :] += xbuf[span, :].astype(F32) + pb[2, span, :]
+
+        row_loop(t, add_first)
+
+    def out(t):
+        span = pl.ds(t * tt, tt)
+        return pltpu.make_async_copy(xbuf.at[span], y_ref.at[span], out_sem.at[t])
+
+    for t in range(parts):
+        zcopy(1, 2, 2, t).wait()
+        last = fetch(2, 1, t)
+        last.start()
+        last.wait()
+
+        def add_last(span):
+            xbuf[span, :] = (pb[0, span, :] + pb[1, span, :]).astype(BF16)
+
+        row_loop(t, add_last)
+        out(t).start()
     for k in (1, 2, 3):
         for p in range(pieces):
             xcopy(k, p).wait_send()
     for k in range(4):
         for j in range(1, 8):
             rcopy(k, j).wait_send()
-    out.wait()
+    for t in range(parts):
+        out(t).wait()
 
 
 def route(ids, gates):
@@ -298,7 +340,7 @@
                 dma((3,)), dma, dma((2,)), dma((2,)),
                 dma((4, pieces)), dma((4, pieces)),
                 dma((4, 8)), dma((4, 8)), dma((4, 8)), dma((4, 8)),
-                dma((3,)), dma((3,)),
+                dma((3, 2)), dma((3, 2)), dma((2,)),
             ],
             compiler_params=pltpu.CompilerParams(has_side_effects=True, vmem_limit_bytes=67043328),
         )(x_loc, ranks, info, w_g[0], w_u[0], w_d[0])

time: 630 us -> 571 us (0.906)
  Pallas kernels: 610 us -> 550 us
    pallas_call x1, Pallas kernels: 610 us -> 550 us  [local_layer(): pl.pallas_call(moe_kernel, out_shape=(jax.ShapeDtypeStruct((tok, hid), BF...]
where the time goes in v2:
time: 571 us; the launch traced here: 570 us
  Pallas kernels  550 us (96%)
  blocking collectives  12.9 us (2%)
    pallas_call x1, Pallas kernels, local_layer(): pl.pallas_call(moe_kernel, out_shape=(jax.ShapeDtypeStruct((tok, hid), BF...  550 us
    all_to_all x1, blocking collectives, route(): return lax.all_to_all(info.transpose(1, 0, 2), 'ez', 0, 0)  12.9 us

profile of v2, /device:TPU:0, one launch (start us, length us, event | category | flops | bytes accessed | tf_op | source)
XLA Modules:
  0.0 569.9 jit_solution(16853073122572008803)
XLA Ops:
  0.0 0.1 stack.131
  0.1 0.8 compare_reduce_fusion
  0.9 0.2 fusion
  1.2 0.8 fusion.1
  2.0 12.9 %all_to_all.5 = f32[4,512,16]{1,2,0:T(8,128)S(1)} all-to-all(f32[4,512,16]{1,2,0:T(8,128)S(1)} %maximum_bitcast_fusion), channel_id=1, replica_groups=mesh['ez'=4,'ey'=2,'ex'=4] {'ez'}, dimensions={0} | all-to-all | bytes 262144 | tf_op jit(solution)/shard_map/all_to_all | solution.py:301
  14.9 0.6 slice_bitcast_fusion.rkr_ref
  15.5 1.3 copy.18.rg_ref
  16.8 549.9 %shard_map.64 = (bf16[512,2048]{1,0:T(8,128)(2,1)}, bf16[3,512,2048]{2,1,0:T(8,128)(2,1)}, bf16[4,1024,2048]{2,1,0:T(8,128)(2,1)}, bf16[4,1024,2048]{2,1,0:T(8,128)(2,1)}, f32[3,512,2048]{2,1,0:T(8,128)}) custom-call(bf16[512,2048]{1,0:T(8,128)(2,1)} %x_ref.1, f32[4,8,512]{2,1,0:T(8,128)} %slice_bitcast_fusion.rkr_ref, f32[4,512,16]{2,1,0:T(8,128)} %copy.18.rg_ref, ...), custom_call_target="tpu_custom_call" | custom-call | tf_op jit(solution)/shard_map/pallas_call | solution.py:318
  566.7 3.2 copy.20
  (1 shorter events, 0.0 us)

commit v3 on v2

--- a/solution.py
+++ b/solution.py
@@ -29,10 +29,10 @@
     return (y + j // 4) % 2, 2 * ((col // 2 + (j // 2) % 2) % 2) + (col % 2 + j % 2) % 2
 
 
-def moe_kernel(x_ref, rkr_ref, rg_ref, w1_ref, w3_ref, w2_ref,
+def moe_kernel(x_ref, rank_ref, info_ref, w1_ref, w3_ref, w2_ref,
                y_ref, xz_ref, dr_ref, rr_ref, zr_ref,
-               w1v, w3v, w2v, gbuf, rbuf, act, xbuf, sel, cmat, pb,
-               w_sem, xl_sem, rl_sem, pl_sem, xs_sem, xr_sem, ds_sem, dr_sem, rs_sem, rc_sem, zs_sem, zr_sem, out_sem):
+               w1v, w3v, w2v, gbuf, rbuf, act, xbuf, sel, cmat, pb, rank_v, info_v,
+               w_sem, xl_sem, rl_sem, pl_sem, xs_sem, xr_sem, ds_sem, dr_sem, rs_sem, rc_sem, zs_sem, zr_sem, out_sem, is_sem, ir_sem):
     tok, hid = x_ref.shape
     ffn = w1_ref.shape[1]
     rows = gbuf.shape[1]
@@ -75,6 +75,22 @@
             src_ref=pb.at[slot, span], dst_ref=zr_ref.at[i, span], send_sem=zs_sem.at[i, t], recv_sem=zr_sem.at[i, t],
             device_id={'ez': z_peer(k)}, device_id_type=MESH)
 
+    def route_copy(own, k, i):
+        src, dst = ((rank_ref, rank_v), (info_ref, info_v))[i]
+        if own:
+            return pltpu.make_async_copy(src.at[z], dst.at[0], ir_sem.at[0, i])
+        peer = z_peer(k)
+        return pltpu.make_async_remote_copy(
+            src_ref=src.at[peer], dst_ref=dst.at[k], send_sem=is_sem.at[k, i], recv_sem=ir_sem.at[k, i],
+            device_id={'ez': peer}, device_id_type=MESH)
+
+    def wait_route(own, k, i):
+        copy = route_copy(own, k, i)
+        if own:
+            copy.wait()
+        else:
+            copy.wait_recv()
+
     def wait_x(k, p):
         span = pl.ds(p * prow, prow)
         pltpu.make_async_remote_copy(
@@ -96,10 +112,11 @@
     def gather(k, own=False):
         load = load_x(own, k)
         load.start()
-        s = z_peer(k)
+        for i in range(2):
+            wait_route(own, k, i)
         for j in range(8):
             slot = lax.broadcasted_iota(jnp.int32, (cap, tok), 0).astype(F32)
-            hit = rkr_ref[s, j:j + 1, :] == slot
+            hit = rank_v[k, j:j + 1, :] == slot
             sel[j * cap:(j + 1) * cap, :] = jnp.where(hit, 1.0, 0.0).astype(BF16)
         load.wait()
 
@@ -150,11 +167,10 @@
             rcopy(k, j).start()
 
     def combine(k, slot, then, done):
-        s = z_peer(k)
         loads = []
         for t in range(parts):
             span = pl.ds(t * tt, tt)
-            info = rg_ref[s, span, :]
+            info = info_v[k, span, :]
             for j in range(8):
                 slots = lax.broadcasted_iota(jnp.int32, (tt, cap), 1).astype(F32)
                 hit = info[:, j:j + 1] == slots
@@ -194,6 +210,12 @@
         span = pl.ds(t * tt, tt)
         return pltpu.make_async_copy(zr_ref.at[i, span], pb.at[slot, span], pl_sem.at[t])
 
+    for i in range(2):
+        route_copy(True, 0, i).start()
+    for k in (1, 2, 3):
+        for i in range(2):
+            route_copy(False, k, i).start()
+
     @pl.when(inner == 0)
     def _():
         for p in range(pieces):
@@ -231,7 +253,13 @@
         return lambda: [send_back(k, h) for h in range(2)] and None
 
     combine(3, 0, back(1), lambda t: zcopy(0, 1, 1, t).start())
-    combine(1, 2, back(2), lambda t: zcopy(2, 0, 1, t).start())
+
+    def send_near(t):
+        @pl.when(inner == 0)
+        def _():
+            zcopy(2, 0, 1, t).start()
+
+    combine(1, 2, back(2), send_near)
 
     def pass_on(t):
         zcopy(0, 1, 1, t).wait()
@@ -250,6 +278,13 @@
     load.start()
     combine(0, 0, lambda: None, lambda t: None)
     load.wait()
+
+    @pl.when(inner == 1)
+    def _():
+        for t in range(parts):
+            zcopy(1, 2, 2, t).wait_send()
+            zcopy(2, 0, 1, t).start()
+
     for t in range(parts):
         zcopy(2, 0, 1, t).wait()
         near = fetch(0, 2, t)
@@ -266,7 +301,12 @@
         return pltpu.make_async_copy(xbuf.at[span], y_ref.at[span], out_sem.at[t])
 
     for t in range(parts):
-        zcopy(1, 2, 2, t).wait()
+        zcopy(1, 2, 2, t).wait_recv()
+
+        @pl.when(inner == 0)
+        def _():
+            zcopy(1, 2, 2, t).wait_send()
+
         last = fetch(2, 1, t)
         last.start()
         last.wait()
@@ -277,6 +317,8 @@
         row_loop(t, add_last)
         out(t).start()
     for k in (1, 2, 3):
+        for i in range(2):
+            route_copy(False, k, i).wait_send()
         for p in range(pieces):
             xcopy(k, p).wait_send()
     for k in range(4):
@@ -298,7 +340,7 @@
     rank = jnp.dot(before, picked.astype(BF16), preferred_element_type=F32)
     rank = jnp.where(picked, rank, -1.0)
     info = jnp.concatenate([rank.reshape(tok, 4, 8), gate.reshape(tok, 4, 8)], axis=2)
-    return lax.all_to_all(info.transpose(1, 0, 2), 'ez', 0, 0)
+    return info.transpose(1, 0, 2)
 
 
 def solution(mesh):
@@ -313,7 +355,6 @@
         ranks = info[:, :, :8].transpose(0, 2, 1)
         pieces = 2
         any_spec = pl.BlockSpec(memory_space=pl.ANY)
-        vmem_spec = pl.BlockSpec(memory_space=pltpu.VMEM)
         dma = pltpu.SemaphoreType.DMA
         outs = pl.pallas_call(
             moe_kernel,
@@ -324,7 +365,7 @@
                 jax.ShapeDtypeStruct((4, rows, hid), BF16),
                 jax.ShapeDtypeStruct((3, tok, hid), F32),
             ),
-            in_specs=[any_spec, vmem_spec, vmem_spec, any_spec, any_spec, any_spec],
+            in_specs=[any_spec] * 6,
             out_specs=(any_spec,) * 5,
             scratch_shapes=[
                 pltpu.VMEM((hid, ffn), BF16),
@@ -337,10 +378,12 @@
                 pltpu.VMEM((rows, tok), BF16),
                 pltpu.VMEM((3, tok // 2, rows), BF16),
                 pltpu.VMEM((3, tok, hid), F32),
+                pltpu.VMEM((4, 8, tok), F32),
+                pltpu.VMEM((4, tok, 16), F32),
                 dma((3,)), dma, dma((2,)), dma((2,)),
                 dma((4, pieces)), dma((4, pieces)),
                 dma((4, 8)), dma((4, 8)), dma((4, 8)), dma((4, 8)),
-                dma((3, 2)), dma((3, 2)), dma((2,)),
+                dma((3, 2)), dma((3, 2)), dma((2,)), dma((4, 2)), dma((4, 2)),
             ],
             compiler_params=pltpu.CompilerParams(has_side_effects=True, vmem_limit_bytes=67043328),
         )(x_loc, ranks, info, w_g[0], w_u[0], w_d[0])

time: 571 us -> 606 us (1.061)
  Pallas kernels: 550 us -> 598 us
  blocking collectives: 12.9 us -> 0 us
    pallas_call x1, Pallas kernels: 550 us -> 598 us  [local_layer(): pl.pallas_call(moe_kernel, out_shape=(jax.ShapeDtypeStruct((tok, hid), BF...]
    all_to_all x1 -> x0, blocking collectives: 12.9 us -> none  [route(): return lax.all_to_all(info.transpose(1, 0, 2), 'ez', 0, 0)]
where the time goes in v3:
time: 606 us; the launch traced here: 605 us
  Pallas kernels  598 us (99%)
    pallas_call x1, Pallas kernels, local_layer(): pl.pallas_call(moe_kernel, out_shape=(jax.ShapeDtypeStruct((tok, hid), BF...  598 us

profile of v3, /device:TPU:0, one launch (start us, length us, event | category | flops | bytes accessed | tf_op | source)
XLA Modules:
  0.0 605.1 jit_solution(72097231617585079)
XLA Ops:
  0.0 0.1 stack.131
  0.1 0.8 compare_reduce_fusion
  0.9 0.2 fusion
  1.2 0.8 fusion.1
  2.0 0.3 copy.19
  2.4 0.0 copy-start
  2.4 1.0 copy-done
  3.3 0.1 slice_bitcast_fusion
  3.4 0.9 copy.20.rank_ref
  4.3 597.6 %shard_map.64 = (bf16[512,2048]{1,0:T(8,128)(2,1)}, bf16[3,512,2048]{2,1,0:T(8,128)(2,1)}, bf16[4,1024,2048]{2,1,0:T(8,128)(2,1)}, bf16[4,1024,2048]{2,1,0:T(8,128)(2,1)}, f32[3,512,2048]{2,1,0:T(8,128)}) custom-call(bf16[512,2048]{1,0:T(8,128)(2,1)} %x_ref.1, f32[4,8,512]{2,1,0:T(8,128)} %copy.20.rank_ref, f32[4,512,16]{2,1,0:T(8,128)} %bitcast.43, ...), custom_call_target="tpu_custom_call" | custom-call | tf_op jit(solution)/shard_map/pallas_call | solution.py:359
  601.9 3.2 copy.22
  (1 shorter events, 0.0 us)
Async XLA Ops:
  2.4 1.0 copy-start
